TPU v7x, 32 devices: a whole 2x2x4 slice. The times are simulated.
32 devices in a mesh: row: 4 (over z), col: 8 (over y, x, core).
Axes of the slice: x: 2, y: 2, z: 4, core: 2. Of those that a mesh axis runs over, the one named last changes fastest.
Arguments:
- coupling: bfloat16 [32768, 32768], P(('row', 'col')), may hold values from -0.0078125 to 0.0078125
- right_side: float32 [32768, 128], P(('row', 'col')), may hold values from -18 to 18
- precond: float32 [128, 256, 256], P(('row', 'col')), may hold values from -0.09375 to 0.09375
Outputs:
- solution: float32 [32768, 128], P(('row', 'col'))
- norms: float32 [4, 128], replicated
All inputs are finite; a program needn't handle non-finite values.
Results may differ from a plain program's by a relative error of at most 0.00082.
Values may be sent and summed in bfloat16 or wider, within the bound.
A program may use at most 128 MiB of HBM per device.

v0:
```python
import jax
import jax.numpy as jnp
from jax import lax
from jax.sharding import PartitionSpec as P

ITERS = 4


def precondition(resid, precond):
    blocks = resid.reshape(precond.shape[0], precond.shape[1], resid.shape[1])
    applied = jnp.einsum("kij,kjn->kin", precond, blocks, precision=lax.Precision.HIGHEST)
    return resid + applied.reshape(resid.shape)


def record_squares(piece, collected):
    squares = jnp.sum(piece * piece, axis=0)
    collected.append(lax.psum(squares, ("row", "col")))


def local(coupling, right_side, precond):
    total = coupling.shape[1]
    collected = []
    solution = jnp.zeros(right_side.shape, jnp.float32)
    for step in range(ITERS):
        if step == 0:
            resid = right_side
        else:
            product = jnp.dot(
                coupling,
                lax.all_gather(solution.astype(jnp.bfloat16), ("row", "col"), axis=0, tiled=True),
                preferred_element_type=jnp.float32,
            )
            resid = right_side - solution - product
        record_squares(resid, collected)
        solution = solution + precondition(resid, precond)
    stacked = jnp.stack(collected)
    norms = jnp.sqrt(stacked / total)
    return (solution, norms)


def solution(mesh):
    in_specs = (P(("row", "col"), None), P(("row", "col"), None), P(("row", "col"), None, None))
    out_specs = (P(("row", "col"), None), P())
    return jax.shard_map(local, mesh=mesh, in_specs=in_specs, out_specs=out_specs, check_vma=False)
```

profile of v0, /device:TPU:0, one launch (start us, length us, event | category | flops | bytes accessed | tf_op | source)
XLA Modules:
  0.0 384.1 jit_solution(8406477353727123377)
XLA Ops:
  7.2 0.0 copy-start
  7.2 0.0 all-gather.4.cloned.1.call-start
  7.2 1.3 copy.5
  8.5 0.0 copy-done
  8.6 2.1 fusion.13
  10.7 0.2 copy.6
  10.9 0.8 fusion.12
  11.7 0.0 all-gather.4.cloned.1.call-update
  11.7 0.0 all-gather.6.cloned.1.call-start
  11.7 80.3 %all-gather.4.cloned.1.call-done = bf16[32768,128]{0,1:T(8,128)(2,1)} async-done(((bf16[1024,128]{0,1:T(8,128)(2,1)}), bf16[32768,128]{0,1:T(8,128)(2,1)}) %all-gather.4.cloned.1.call-update) | async-done | bytes 8388624 | tf_op jit(solution)/shard_map/all_gather | solution.py:30
  92.0 28.3 %fusion = f32[1024,128]{0,1:T(8,128)S(1)} fusion(bf16[32768,128]{0,1:T(8,128)(2,1)} %all-gather.4.cloned.1.call-done, bf16[1024,32768]{1,0:T(8,128)(2,1)} %param.3, f32[1024,128]{0,1:T(8,128)S(1)} %copy.5, f32[1024,128]{0,1:T(8,128)S(1)} %get-tuple-element.13), kind=kOutput, calls=%fused_computation.6 | convolution fusion | flops 8590196736 | bytes 77070336 | tf_op jit(solution)/shard_map/dot_general | solution.py:28
  120.3 1.2 convolution_bitcast_fusion.2
  121.5 0.8 fusion.11
  122.3 0.0 all-gather.6.cloned.1.call-update
  122.3 0.0 all-gather.8.cloned.1.call-start
  122.4 76.8 %all-gather.6.cloned.1.call-done = bf16[32768,128]{0,1:T(8,128)(2,1)} async-done(((bf16[1024,128]{0,1:T(8,128)(2,1)}), bf16[32768,128]{0,1:T(8,128)(2,1)}) %all-gather.6.cloned.1.call-update) | async-done | bytes 8388624 | tf_op jit(solution)/shard_map/all_gather | solution.py:30
  199.2 28.3 %fusion.1 = f32[1024,128]{0,1:T(8,128)S(1)} fusion(bf16[32768,128]{0,1:T(8,128)(2,1)} %all-gather.6.cloned.1.call-done, bf16[1024,32768]{1,0:T(8,128)(2,1)} %param.3, f32[1024,128]{0,1:T(8,128)S(1)} %copy.5, f32[1024,128]{0,1:T(8,128)S(1)} %get-tuple-element.11), kind=kOutput, calls=%fused_computation.7 | convolution fusion | flops 8590196736 | bytes 77070336 | tf_op jit(solution)/shard_map/dot_general | solution.py:28
  227.5 1.2 convolution_bitcast_fusion.1
  228.7 0.8 fusion.10
  229.5 0.0 all-gather.8.cloned.1.call-update
  229.5 1.2 multiply_reduce_fusion.3
  230.7 75.7 %all-gather.8.cloned.1.call-done = bf16[32768,128]{0,1:T(8,128)(2,1)} async-done(((bf16[1024,128]{0,1:T(8,128)(2,1)}), bf16[32768,128]{0,1:T(8,128)(2,1)}) %all-gather.8.cloned.1.call-update) | async-done | bytes 8388624 | tf_op jit(solution)/shard_map/all_gather | solution.py:30
  306.4 28.3 %fusion.2 = f32[1024,128]{0,1:T(8,128)S(1)} fusion(bf16[32768,128]{0,1:T(8,128)(2,1)} %all-gather.8.cloned.1.call-done, bf16[1024,32768]{1,0:T(8,128)(2,1)} %param.3, f32[1024,128]{0,1:T(8,128)S(1)} %copy.5, f32[1024,128]{0,1:T(8,128)S(1)} %get-tuple-element.9), kind=kOutput, calls=%fused_computation.8 | convolution fusion | flops 8590196736 | bytes 77070336 | tf_op jit(solution)/shard_map/dot_general | solution.py:28
  334.7 1.2 convolution_bitcast_fusion
  335.9 0.2 multiply_reduce_fusion
  336.0 1.0 copy.16
  337.0 39.9 %all-reduce = (f32[1,128]{1,0:T(1,128)S(1)}, f32[1,128]{1,0:T(1,128)S(1)}, f32[1,128]{1,0:T(1,128)S(1)}, f32[1,128]{1,0:T(1,128)S(1)}) all-reduce(f32[1,128]{1,0:T(1,128)S(1)} %bitcast.64, f32[1,128]{1,0:T(1,128)S(1)} %bitcast.62, f32[1,128]{1,0:T(1,128)S(1)} %bitcast.61, ...), channel_id=1, replica_groups=mesh['row'=4,'col'=8] {'row','col'}, use_global_device_ids=true, to_apply=%region_7.0 | all-reduce | flops 512 | bytes 4096 | tf_op jit(solution)/shard_map/psum | solution.py:17
  377.0 0.6 fusion.9
  (3 shorter events, 0.1 us)
Async XLA Ops:
  7.2 1.4 copy-start
  7.2 84.8 %all-gather.4.cloned.1.call-start = ((), (), s32[]{:S(2)}) async-start(), calls=%async_computation | async-start | bytes 8650752 | tf_op jit(solution)/shard_map/all_gather | solution.py:30
  11.7 187.5 %all-gather.6.cloned.1.call-start = ((), (), s32[]{:S(2)}) async-start(), calls=%async_computation.1 | async-start | bytes 8650752 | tf_op jit(solution)/shard_map/all_gather | solution.py:30
  122.3 184.0 %all-gather.8.cloned.1.call-start = ((), (), s32[]{:S(2)}) async-start(), calls=%async_computation.2 | async-start | bytes 8650752 | tf_op jit(solution)/shard_map/all_gather | solution.py:30
Sparse Core Ops, SparseCore 0:
  11.8 80.1 all-gather.3
  122.5 76.6 all-gather.5
  229.6 76.6 all-gather.7
where the time goes:
time: 385 us; the launch traced here: 384 us
  waiting for transfers between devices  233 us (61%)
  matrix products  90.4 us (23%)
  blocking collectives  39.9 us (10%)
  between operations  13.9 us (4%)
  other arithmetic  4.32 us (1%)
    all_gather x3, waiting for transfers between devices, local(): lax.all_gather(solution.astype(jnp.bfloat16), ('row', 'col'), axis=0, til...  233 us
    dot_general x3, matrix products, local(): jnp.dot(coupling, lax.all_gather(solution.astype(jnp.bfloat16), ('row', '...  84.9 us
    psum x1, blocking collectives, record_squares(): collected.append(lax.psum(squares, ('row', 'col')))  39.9 us
  transfers between devices with their start and end apart: 3, of which 3 were waited for; matrix products, arithmetic and copies ran while one was open for 0% of the time, Pallas kernels for 0%

commit v1 on v0

v1 whole, which is shorter than its diff:
```python
import functools

import jax
import jax.numpy as jnp
from jax import lax
from jax.experimental import pallas as pl
from jax.experimental.pallas import tpu as pltpu
from jax.sharding import PartitionSpec as P

ITERS = 4
CORES = 2
INNER = 2


def precondition(resid, precond):
    blocks = resid.reshape(precond.shape[0], precond.shape[1], resid.shape[1])
    applied = jnp.einsum("kij,kjn->kin", precond, blocks, precision=lax.Precision.HIGHEST)
    return resid + applied.reshape(resid.shape)


def plan(rows_axis, cols_axis):
    outer = cols_axis // (CORES * INNER)
    plane = [("z", k, 0, 0) for k in range(1, rows_axis)]
    for k in range(rows_axis):
        plane += [("a", k, i, 0) for i in range(1, outer)] + [("b", k, 0, j) for j in range(1, INNER)]
        plane += [(d, k, i, j) for d in "pq" for i in range(1, outer) for j in range(1, INNER)]
    every = plane + [("own", 0, 0, 0)]
    return every + [("core",) + name for name in every]


def gather_kernel(rows_axis, cols_axis, x_ref, out_ref, send_sem, recv_sem):
    outer = cols_axis // (CORES * INNER)
    r, c = lax.axis_index("row"), lax.axis_index("col")
    core, chip = lax.rem(c, CORES), lax.div(c, CORES)
    b, a = lax.rem(chip, INNER), lax.div(chip, INNER)
    rows = x_ref.shape[0]
    half = rows // 2
    number = {name: at for at, name in enumerate(plan(rows_axis, cols_axis))}

    def back(v, k, size):
        return lax.rem(v + size - k, size)

    def ahead(v, k, size):
        return lax.rem(v + k, size)

    def device(r, a, b, core):
        return (r, (a * INNER + b) * CORES + core)

    def shard(k, i, j, part=None, core=core):
        index = back(r, k, rows_axis) * cols_axis + (back(a, i, outer) * INNER + back(b, j, INNER)) * CORES + core
        start, size = index * rows, rows
        if part is not None:
            start, size = start + part * half, half
        return out_ref.at[pl.ds(pl.multiple_of(start, size), size), :]

    peers = [device(ahead(r, k, rows_axis), a, b, core) for k in range(1, rows_axis)]
    over_a = [device(r, ahead(a, i, outer), b, core) for i in range(1, outer)]
    over_b = [device(r, a, ahead(b, j, INNER), core) for j in range(1, INNER)]
    partner = device(r, a, b, 1 - core)

    barrier = pltpu.get_barrier_semaphore()
    everyone = peers + over_a + over_b + [partner]
    for peer in everyone:
        pl.semaphore_signal(barrier, inc=1, device_id=peer, device_id_type=pl.DeviceIdType.MESH)
    pl.semaphore_wait(barrier, len(everyone))

    sent = []

    def copy(src, dst, name, to):
        at = number[name]
        return pltpu.make_async_remote_copy(
            src_ref=src,
            dst_ref=dst,
            send_sem=send_sem.at[at],
            recv_sem=recv_sem.at[at],
            device_id=to,
            device_id_type=pl.DeviceIdType.MESH,
        )

    def send(src, dst, name, to):
        moved = copy(src, dst, name, to)
        moved.start()
        sent.append(moved)

    def arrive(ref, name):
        copy(ref, ref, name, partner).wait_recv()

    def spread(k, src, dst):
        for i in range(1, outer):
            send(src, dst, ("a", k, i, 0), over_a[i - 1])
        for j in range(1, INNER):
            send(src, dst, ("b", k, 0, j), over_b[j - 1])

    mine = shard(0, 0, 0)
    spread(0, x_ref, mine)
    for k in range(1, rows_axis):
        send(x_ref, mine, ("z", k, 0, 0), peers[k - 1])
    send(x_ref, mine, ("core", "own", 0, 0, 0), partner)
    index = r * cols_axis + c
    out_ref[pl.ds(pl.multiple_of(index * rows, rows), rows), :] = x_ref[...]

    for k in range(1, rows_axis):
        ref = shard(k, 0, 0)
        arrive(ref, ("z", k, 0, 0))
        spread(k, ref, ref)
        send(ref, ref, ("core", "z", k, 0, 0), partner)
    for k in range(rows_axis):
        for i in range(1, outer):
            ref = shard(k, i, 0)
            arrive(ref, ("a", k, i, 0))
            for j in range(1, INNER):
                send(shard(k, i, 0, 0), shard(k, i, 0, 0), ("p", k, i, j), over_b[j - 1])
            send(ref, ref, ("core", "a", k, i, 0), partner)
        for j in range(1, INNER):
            ref = shard(k, 0, j)
            arrive(ref, ("b", k, 0, j))
            for i in range(1, outer):
                send(shard(k, 0, j, 1), shard(k, 0, j, 1), ("q", k, i, j), over_a[i - 1])
            send(ref, ref, ("core", "b", k, 0, j), partner)
    for k in range(rows_axis):
        for i in range(1, outer):
            for j in range(1, INNER):
                for part, kind in ((0, "p"), (1, "q")):
                    ref = shard(k, i, j, part)
                    arrive(ref, (kind, k, i, j))
                    send(ref, ref, ("core", kind, k, i, j), partner)

    other = 1 - core
    for name in number:
        if name[0] == "core":
            kind, k, i, j = name[1:]
            part = {"p": 0, "q": 1}.get(kind)
            arrive(shard(k, i, j, part, other), name)
    for moved in sent:
        moved.wait_send()


def gather(x, rows_axis, cols_axis, number):
    copies = len(plan(rows_axis, cols_axis))
    total = rows_axis * cols_axis * x.shape[0]
    return pl.pallas_call(
        functools.partial(gather_kernel, rows_axis, cols_axis),
        out_shape=jax.ShapeDtypeStruct((total, x.shape[1]), x.dtype),
        in_specs=[pl.BlockSpec(memory_space=pltpu.VMEM)],
        out_specs=pl.BlockSpec(memory_space=pltpu.VMEM),
        scratch_shapes=[pltpu.SemaphoreType.DMA((copies,)), pltpu.SemaphoreType.DMA((copies,))],
        compiler_params=pltpu.CompilerParams(collective_id=number, has_side_effects=True),
    )(x)


def local(rows_axis, cols_axis, coupling, right_side, precond):
    total = coupling.shape[1]
    collected = []
    solution = jnp.zeros(right_side.shape, jnp.float32)
    for step in range(ITERS):
        if step == 0:
            resid = right_side
        else:
            everyone = gather(solution.astype(jnp.bfloat16), rows_axis, cols_axis, 0)
            product = jnp.dot(coupling, everyone, preferred_element_type=jnp.float32)
            resid = right_side - solution - product
        collected.append(jnp.sum(resid * resid, axis=0))
        solution = solution + precondition(resid, precond)
    squares = jnp.pad(jnp.stack(collected), ((0, 16 - ITERS), (0, 0)))
    squares = gather(squares, rows_axis, cols_axis, 1).reshape(-1, 16, squares.shape[1])
    norms = jnp.sqrt(jnp.sum(squares[:, :ITERS], axis=0) / total)
    return (solution, norms)


def solution(mesh):
    in_specs = (P(("row", "col"), None), P(("row", "col"), None), P(("row", "col"), None, None))
    out_specs = (P(("row", "col"), None), P())
    body = functools.partial(local, mesh.shape["row"], mesh.shape["col"])
    return jax.shard_map(body, mesh=mesh, in_specs=in_specs, out_specs=out_specs, check_vma=False)
```

time: 385 us -> 289 us (0.75)
  waiting for transfers between devices: 233 us -> 0 us
  Pallas kernels: 0 us -> 185 us
  blocking collectives: 39.9 us -> 0 us
  between operations: 13.9 us -> 0.78 us
  other arithmetic: 4.32 us -> 8.58 us
    all_gather x3 -> x0, waiting for transfers between devices: 233 us -> none  [local(): lax.all_gather(solution.astype(jnp.bfloat16), ('row', 'col'), axis=0, til...]
    pallas_call x0 -> x4, Pallas kernels: none -> 185 us  [gather(): pl.pallas_call(functools.partial(gather_kernel, rows_axis, cols_axis), ou...]
    psum x1 -> x0, blocking collectives: 39.9 us -> none  [record_squares(): collected.append(lax.psum(squares, ('row', 'col')))]
  transfers between devices with their start and end apart: 3 -> 0, of which waited for: 3 -> 0; matrix products, arithmetic and copies ran while one was open for 0% -> 0% of each run, Pallas kernels for 0% -> 0%
where the time goes in v1:
time: 289 us
  Pallas kernels  185 us (64%)
  matrix products  90.9 us (31%)
  other arithmetic  8.58 us (3%)
  local copies, waits for them, and re-layouts  3.62 us (1%)
    pallas_call x4, Pallas kernels, gather(): pl.pallas_call(functools.partial(gather_kernel, rows_axis, cols_axis), ou...  185 us
    dot_general x3, matrix products, local(): product = jnp.dot(coupling, everyone, preferred_element_type=jnp.float32)  84.3 us
    dot_general x4, matrix products, precondition(): jnp.einsum('kij,kjn->kin', precond, blocks, precision=lax.Precision.HIGHEST)  6.65 us

profile of v1, /device:TPU:0, one launch (start us, length us, event | category | flops | bytes accessed | tf_op | source)
XLA Modules:
  0.0 288.8 jit_solution(5221790284084464723)
XLA Ops:
  0.6 0.0 copy-start
  0.6 0.0 copy-start.1
  0.7 1.2 copy-done
  1.9 2.1 fusion.11
  4.0 1.8 bitcast_add_fusion.3
  5.8 52.9 %shard_map.50 = bf16[32768,128]{1,0:T(8,128)(2,1)} custom-call(bf16[1024,128]{1,0:T(8,128)(2,1)} %get-tuple-element.7.x_ref), custom_call_target="tpu_custom_call" | custom-call | tf_op jit(solution)/shard_map/pallas_call | solution.py:141
  58.6 0.0 copy-done.1
  58.7 28.0 %fusion = f32[1024,128]{1,0:T(8,128)S(1)} fusion(bf16[1024,32768]{1,0:T(8,128)(2,1)} %param.3, bf16[32768,128]{1,0:T(8,128)(2,1)} %shard_map.50, f32[1024,128]{1,0:T(8,128)S(1)} %copy-done.1, f32[1024,128]{1,0:T(8,128)S(1)} %get-tuple-element.6), kind=kOutput, calls=%fused_computation.6 | convolution fusion | flops 8590196736 | bytes 77070336 | tf_op jit(solution)/shard_map/dot_general | solution.py:160
  86.7 0.0 copy-start.3
  86.7 0.8 copy-done.3
  87.5 1.3 convolution_bitcast_fusion.2
  88.7 0.2 copy.7
  88.9 1.9 fusion.9
  90.8 57.1 %shard_map.51 = bf16[32768,128]{1,0:T(8,128)(2,1)} custom-call(bf16[1024,128]{1,0:T(8,128)(2,1)} %get-tuple-element.4.x_ref), custom_call_target="tpu_custom_call" | custom-call | tf_op jit(solution)/shard_map/pallas_call | solution.py:141
  147.9 28.2 %fusion.1 = f32[1024,128]{1,0:T(8,128)S(1)} fusion(bf16[1024,32768]{1,0:T(8,128)(2,1)} %param.3, bf16[32768,128]{1,0:T(8,128)(2,1)} %shard_map.51, f32[1024,128]{1,0:T(8,128)S(1)} %copy-done.1, f32[1024,128]{1,0:T(8,128)S(1)} %get-tuple-element.5), kind=kOutput, calls=%fused_computation.7 | convolution fusion | flops 8590196736 | bytes 77070336 | tf_op jit(solution)/shard_map/dot_general | solution.py:160
  176.1 0.0 copy-start.2
  176.1 2.0 convolution_bitcast_fusion.1
  178.2 0.0 copy-done.2
  178.2 1.2 copy.10
  179.4 1.8 fusion.7
  181.3 55.6 %shard_map.52 = bf16[32768,128]{1,0:T(8,128)(2,1)} custom-call(bf16[1024,128]{1,0:T(8,128)(2,1)} %get-tuple-element.2.x_ref), custom_call_target="tpu_custom_call" | custom-call | tf_op jit(solution)/shard_map/pallas_call | solution.py:141
  236.9 28.0 %fusion.2 = f32[1024,128]{1,0:T(8,128)S(1)} fusion(bf16[1024,32768]{1,0:T(8,128)(2,1)} %param.3, bf16[32768,128]{1,0:T(8,128)(2,1)} %shard_map.52, f32[1024,128]{1,0:T(8,128)S(1)} %copy-done.1, f32[1024,128]{1,0:T(8,128)S(1)} %get-tuple-element.3), kind=kOutput, calls=%fused_computation.8 | convolution fusion | flops 8590196736 | bytes 77070336 | tf_op jit(solution)/shard_map/dot_general | solution.py:160
  264.9 1.3 convolution_bitcast_fusion
  266.2 0.2 copy.13
  266.4 0.9 multiply_reduce_fusion
  267.2 0.6 select_maximum_fusion.x_ref
  267.8 19.4 %shard_map.53 = f32[512,128]{1,0:T(8,128)} custom-call(f32[16,128]{1,0:T(8,128)} %select_maximum_fusion.x_ref), custom_call_target="tpu_custom_call" | custom-call | tf_op jit(solution)/shard_map/pallas_call | solution.py:141
  287.3 0.9 slice_reduce_fusion
  288.2 0.6 multiply_sqrt_fusion
Async XLA Ops:
  0.6 1.2 copy-start
  0.6 58.0 %copy-start.1 = (f32[1024,128]{1,0:T(8,128)S(1)}, f32[1024,128]{1,0:T(8,128)}, u32[]{:S(2)}) copy-start(f32[1024,128]{1,0:T(8,128)} %param.4) | copy-start | bytes 1572868
  86.7 0.8 copy-start.3
  176.1 2.1 copy-start.2

commit v2 on v1

--- a/solution.py
+++ b/solution.py
@@ -99,12 +99,7 @@
     index = r * cols_axis + c
     out_ref[pl.ds(pl.multiple_of(index * rows, rows), rows), :] = x_ref[...]
 
-    for k in range(1, rows_axis):
-        ref = shard(k, 0, 0)
-        arrive(ref, ("z", k, 0, 0))
-        spread(k, ref, ref)
-        send(ref, ref, ("core", "z", k, 0, 0), partner)
-    for k in range(rows_axis):
+    def cross(k):
         for i in range(1, outer):
             ref = shard(k, i, 0)
             arrive(ref, ("a", k, i, 0))
@@ -117,6 +112,14 @@
             for i in range(1, outer):
                 send(shard(k, 0, j, 1), shard(k, 0, j, 1), ("q", k, i, j), over_a[i - 1])
             send(ref, ref, ("core", "b", k, 0, j), partner)
+
+    for k in range(1, rows_axis):
+        ref = shard(k, 0, 0)
+        arrive(ref, ("z", k, 0, 0))
+        spread(k, ref, ref)
+        send(ref, ref, ("core", "z", k, 0, 0), partner)
+        cross(k - 1)
+    cross(rows_axis - 1)
     for k in range(rows_axis):
         for i in range(1, outer):
             for j in range(1, INNER):

time: 289 us -> 284 us (0.983)
  Pallas kernels: 185 us -> 179 us
    pallas_call x4, Pallas kernels: 185 us -> 179 us  [gather(): pl.pallas_call(functools.partial(gather_kernel, rows_axis, cols_axis), ou...]
where the time goes in v2:
time: 284 us; the launch traced here: 283 us
  Pallas kernels  179 us (63%)
  matrix products  90.9 us (32%)
  other arithmetic  8.58 us (3%)
  local copies, waits for them, and re-layouts  3.62 us (1%)
    pallas_call x4, Pallas kernels, gather(): pl.pallas_call(functools.partial(gather_kernel, rows_axis, cols_axis), ou...  179 us
    dot_general x3, matrix products, local(): product = jnp.dot(coupling, everyone, preferred_element_type=jnp.float32)  84.3 us
    dot_general x4, matrix products, precondition(): jnp.einsum('kij,kjn->kin', precond, blocks, precision=lax.Precision.HIGHEST)  6.65 us

profile of v2, /device:TPU:0, one launch (start us, length us, event | category | flops | bytes accessed | tf_op | source)
XLA Modules:
  0.0 282.9 jit_solution(8058553917925808540)
XLA Ops:
  0.6 0.0 copy-start
  0.6 0.0 copy-start.1
  0.7 1.2 copy-done
  1.9 2.1 fusion.11
  4.0 1.8 bitcast_add_fusion.3
  5.8 51.0 %shard_map.50 = bf16[32768,128]{1,0:T(8,128)(2,1)} custom-call(bf16[1024,128]{1,0:T(8,128)(2,1)} %get-tuple-element.7.x_ref), custom_call_target="tpu_custom_call" | custom-call | tf_op jit(solution)/shard_map/pallas_call | solution.py:144
  56.8 0.0 copy-done.1
  56.8 28.0 %fusion = f32[1024,128]{1,0:T(8,128)S(1)} fusion(bf16[1024,32768]{1,0:T(8,128)(2,1)} %param.3, bf16[32768,128]{1,0:T(8,128)(2,1)} %shard_map.50, f32[1024,128]{1,0:T(8,128)S(1)} %copy-done.1, f32[1024,128]{1,0:T(8,128)S(1)} %get-tuple-element.6), kind=kOutput, calls=%fused_computation.6 | convolution fusion | flops 8590196736 | bytes 77070336 | tf_op jit(solution)/shard_map/dot_general | solution.py:163
  84.8 0.0 copy-start.3
  84.9 0.8 copy-done.3
  85.6 1.2 convolution_bitcast_fusion.2
  86.9 0.2 copy.7
  87.1 1.9 fusion.9
  89.0 52.9 %shard_map.51 = bf16[32768,128]{1,0:T(8,128)(2,1)} custom-call(bf16[1024,128]{1,0:T(8,128)(2,1)} %get-tuple-element.4.x_ref), custom_call_target="tpu_custom_call" | custom-call | tf_op jit(solution)/shard_map/pallas_call | solution.py:144
  141.9 28.2 %fusion.1 = f32[1024,128]{1,0:T(8,128)S(1)} fusion(bf16[1024,32768]{1,0:T(8,128)(2,1)} %param.3, bf16[32768,128]{1,0:T(8,128)(2,1)} %shard_map.51, f32[1024,128]{1,0:T(8,128)S(1)} %copy-done.1, f32[1024,128]{1,0:T(8,128)S(1)} %get-tuple-element.5), kind=kOutput, calls=%fused_computation.7 | convolution fusion | flops 8590196736 | bytes 77070336 | tf_op jit(solution)/shard_map/dot_general | solution.py:163
  170.1 0.0 copy-start.2
  170.1 2.0 convolution_bitcast_fusion.1
  172.1 0.0 copy-done.2
  172.1 1.2 copy.10
  173.4 1.8 fusion.7
  175.2 53.8 %shard_map.52 = bf16[32768,128]{1,0:T(8,128)(2,1)} custom-call(bf16[1024,128]{1,0:T(8,128)(2,1)} %get-tuple-element.2.x_ref), custom_call_target="tpu_custom_call" | custom-call | tf_op jit(solution)/shard_map/pallas_call | solution.py:144
  229.0 28.0 %fusion.2 = f32[1024,128]{1,0:T(8,128)S(1)} fusion(bf16[1024,32768]{1,0:T(8,128)(2,1)} %param.3, bf16[32768,128]{1,0:T(8,128)(2,1)} %shard_map.52, f32[1024,128]{1,0:T(8,128)S(1)} %copy-done.1, f32[1024,128]{1,0:T(8,128)S(1)} %get-tuple-element.3), kind=kOutput, calls=%fused_computation.8 | convolution fusion | flops 8590196736 | bytes 77070336 | tf_op jit(solution)/shard_map/dot_general | solution.py:163
  257.1 1.3 convolution_bitcast_fusion
  258.3 0.2 copy.13
  258.5 0.9 multiply_reduce_fusion
  259.4 0.6 select_maximum_fusion.x_ref
  260.0 21.4 %shard_map.53 = f32[512,128]{1,0:T(8,128)} custom-call(f32[16,128]{1,0:T(8,128)} %select_maximum_fusion.x_ref), custom_call_target="tpu_custom_call" | custom-call | tf_op jit(solution)/shard_map/pallas_call | solution.py:144
  281.4 0.9 slice_reduce_fusion
  282.3 0.6 multiply_sqrt_fusion
Async XLA Ops:
  0.6 1.2 copy-start
  0.6 56.2 %copy-start.1 = (f32[1024,128]{1,0:T(8,128)S(1)}, f32[1024,128]{1,0:T(8,128)}, u32[]{:S(2)}) copy-start(f32[1024,128]{1,0:T(8,128)} %param.4) | copy-start | bytes 1572868
  84.8 0.8 copy-start.3
  170.1 2.1 copy-start.2
